TPU v7x, 256 devices: a whole 4x4x8 slice. The times are simulated.
256 devices in a mesh: tile: 64 (over z, y_hi, x), sub: 4 (over y_lo, core).
Axes of the slice: x: 4, y: 4 (y_hi: 2, y_lo: 2; y = y_hi * 2 + y_lo), z: 8, core: 2. Of those that a mesh axis runs over, the one named last changes fastest.
Arguments:
- grid_feats: bfloat16 [32768, 512], P(('tile', 'sub')), may hold values from -6 to 6
- mesh_feats: bfloat16 [32768, 512], P(('tile', 'sub')), may hold values from -6 to 6
- encode_edges: bfloat16 [262144, 512], P(('tile', 'sub')), may hold values from -6 to 6
- decode_edges: bfloat16 [131072, 512], P(('tile', 'sub')), may hold values from -6 to 6
- encode_source: int32 [262144], P(('tile', 'sub')), may hold values from 0 to 32767, as said below
- encode_target: int32 [262144], P(('tile', 'sub')), may hold values from -1 to 32767, as said below
- decode_source: int32 [131072], P(('tile', 'sub')), may hold values from 0 to 32767, as said below
- decode_target: int32 [131072], P(('tile', 'sub')), may hold values from -1 to 32767, as said below
- owner_fine: int32 [32768], P(('tile', 'sub')), may hold values from 0 to 8191, as said below
- owner_coarse: int32 [8192], P('tile'), may hold values from 0 to 511
- encode_weight: bfloat16 [512, 512], replicated, may hold values from -0.25 to 0.25
- decode_weight: bfloat16 [512, 512], replicated, may hold values from -0.25 to 0.25
- middle_weight: bfloat16 [512, 512], replicated, may hold values from -0.25 to 0.25
- summit_weight: bfloat16 [512, 512], replicated, may hold values from -0.25 to 0.25
- cotangent: bfloat16 [32768, 512], P(('tile', 'sub')), may hold values from -6 to 6
Outputs:
- grid_update: bfloat16 [32768, 512], P(('tile', 'sub'))
- encode_grad: float32 [512, 512], replicated
- decode_grad: float32 [512, 512], replicated
- middle_grad: float32 [512, 512], replicated
- summit_grad: float32 [512, 512], replicated
Inputs may be any that keep to these rules, and one draw needn't show every extreme that they name: `encode_source`: edge slot e is listed on device d = e // 1024; its source grid node lies on device d - 1, d or d + 1. `encode_target`: -1 marks padding; every other value is a mesh node of the device that lists the slot. On each device padding fills whole blocks of 128 slots after all live ones; every device has a live block, and some device has no padding. `decode_source`: edge slot e is listed on device d = e // 512; its source mesh node lies on device d - 1, d or d + 1. `decode_target`: -1 marks padding; every other value is a grid node of the device that lists the slot. On each device padding fills whole blocks of 128 slots after all live ones; every device has a live block, and some device has no padding. `owner_fine`: the middle node of fine mesh node m lies on the tile of the device that holds m.
All inputs are finite; a program needn't handle non-finite values.
Results may differ from a plain program's by a relative error of at most 0.012.
Values may be sent and summed in bfloat16 or wider, within the bound.
A program may use at most 64 MiB of HBM per device.

v0:
```python
import jax
import jax.numpy as jnp
from jax import lax
from jax.sharding import PartitionSpec as P

TOP_NODES = 512
BLOCK = 128


def with_halo(x, sides, width):
    edges = {}
    for axis, dim in sides:
        peers, length = (lax.axis_size(axis), x.shape[dim])
        up = [(i, (i + 1) % peers) for i in range(peers - 1)]
        last = lax.slice_in_dim(x, length - width, length, axis=dim)
        initial = lax.slice_in_dim(x, 0, width, axis=dim)
        edges[dim] = (
            lax.ppermute(last, axis, up),
            lax.ppermute(initial, axis, [(b, a) for a, b in up]),
        )
    done = []
    for _, dim in sides:
        low, high = edges[dim]
        around = [(width, width) if d in done else (0, 0) for d in range(x.ndim)]
        x = jnp.concatenate([jnp.pad(low, around), x, jnp.pad(high, around)], axis=dim)
        done.append(dim)
    return x


def copy_for_each(x, axis):
    peers = lax.axis_size(axis)
    return lax.all_to_all(jnp.broadcast_to(x[None], (peers, *x.shape)), axis, 0, 0, tiled=True)


def taken_together(x, axis):
    return copy_for_each(x, axis).sum(axis=0)


def split_up(x, dim, peers):
    dims = x.shape
    pieces = x.reshape(*dims[:dim], peers, dims[dim] // peers, *dims[dim + 1 :])
    return jnp.moveaxis(pieces, dim, 0)


def summed_on_arrival(x, axis, dim):
    pieces = split_up(x, dim, lax.axis_size(axis))
    arrived = lax.all_to_all(pieces, axis, split_axis=0, concat_axis=0, tiled=True)
    return arrived.sum(axis=0)


def joined_along(pieces, dim):
    dims = list(pieces.shape[1:])
    dims[dim] *= pieces.shape[0]
    return jnp.moveaxis(pieces, 0, dim).reshape(dims)


def gather_directly(x, axis, dim):
    return joined_along(copy_for_each(x, axis), dim)


def from_behind(x, axis, by):
    peers = lax.axis_size(axis)
    pairs = [(i, i + by) for i in range(peers) if 0 <= i + by < peers]
    return lax.ppermute(x, axis, pairs)


def silu_slope(values):
    sigmoid = jax.nn.sigmoid(values)
    return sigmoid * (1.0 + values * (1.0 - sigmoid))


def live_count(targets):
    heads = targets.reshape(-1, BLOCK)[:, 0]
    return jnp.sum((heads >= 0).astype(jnp.int32))


def local_targets(targets, first, limit):
    return jnp.where(targets >= 0, targets - first, limit)


def outer_sum(left, right):
    return lax.dot_general(
        left, right, (((0,), (0,)), ((), ())), preferred_element_type=jnp.float32
    )


def times_transposed(left, right):
    return lax.dot_general(
        left, right, (((1,), (1,)), ((), ())), preferred_element_type=jnp.float32
    )


def membership(indices, rows, dtype):
    return (jnp.arange(rows, dtype=jnp.int32)[:, None] == indices[None, :]).astype(dtype)


def exact_sum(members, values):
    return jnp.dot(
        members, values, precision=lax.Precision.HIGHEST, preferred_element_type=jnp.float32
    )


def edge_forward(sources, senders, targets, edge_feats, weight, segments, blocks):
    features = weight.shape[1]

    def block_step(block_id, carried):
        summed, stored = carried
        offset = block_id * BLOCK
        picked = lax.dynamic_slice_in_dim(senders, offset, BLOCK)
        receivers = lax.dynamic_slice_in_dim(targets, offset, BLOCK)
        edge_part = lax.dynamic_slice_in_dim(edge_feats, offset, BLOCK, 0)
        fetched = jnp.take(sources, picked, axis=0)
        preact = jnp.dot(fetched, weight, preferred_element_type=jnp.float32) + edge_part.astype(
            jnp.float32
        )
        summed = summed + exact_sum(
            membership(receivers, segments, jnp.float32), jax.nn.silu(preact)
        )
        stored = lax.dynamic_update_slice_in_dim(stored, preact, offset, 0)
        return (summed, stored)

    start_sum = jnp.zeros((segments, features), jnp.float32)
    start_store = jnp.zeros((senders.shape[0], features), jnp.float32)
    return lax.fori_loop(0, blocks, block_step, (start_sum, start_store))


def edge_backward(
    sources, senders, targets, stored, weight, upstream, factor, blocks, returned_rows
):
    features = weight.shape[1]

    def block_step(block_id, carried):
        gradient, returned = carried
        offset = block_id * BLOCK
        picked = lax.dynamic_slice_in_dim(senders, offset, BLOCK)
        receivers = lax.dynamic_slice_in_dim(targets, offset, BLOCK)
        preact = lax.dynamic_slice_in_dim(stored, offset, BLOCK, 0)
        fetched = jnp.take(sources, picked, axis=0)
        incoming = jnp.take(upstream, receivers, axis=0).astype(jnp.float32) * factor
        slope = (incoming * silu_slope(preact)).astype(jnp.bfloat16)
        gradient = gradient + outer_sum(fetched, slope)
        if returned_rows:
            passed = times_transposed(slope, weight)
            returned = returned + exact_sum(membership(picked, returned_rows, jnp.float32), passed)
        return (gradient, returned)

    start_grad = jnp.zeros((features, features), jnp.float32)
    start_back = jnp.zeros((max(returned_rows, 1), features), jnp.float32)
    return lax.fori_loop(0, blocks, block_step, (start_grad, start_back))


def shards(
    grid_feats,
    mesh_feats,
    encode_edges,
    decode_edges,
    encode_source,
    encode_target,
    decode_source,
    decode_target,
    owner_fine,
    owner_coarse,
    encode_weight,
    decode_weight,
    middle_weight,
    summit_weight,
    cotangent,
):
    grid_rows = grid_feats.shape[0]
    mesh_rows = mesh_feats.shape[0]
    level_rows = owner_coarse.shape[0]
    tiles = lax.axis_size("tile")
    subs = lax.axis_size("sub")
    device = lax.axis_index(("tile", "sub"))
    tile_id = lax.axis_index("tile")
    encode_factor = mesh_rows / encode_source.shape[0]
    decode_factor = grid_rows / decode_source.shape[0]
    middle_factor = level_rows / (mesh_rows * subs)
    summit_factor = TOP_NODES / (level_rows * tiles)
    grid_wide = with_halo(grid_feats, ((("tile", "sub"), 0),), grid_rows)
    encode_senders = encode_source - (device - 1) * grid_rows
    encode_targets = local_targets(encode_target, device * mesh_rows, mesh_rows)
    encode_blocks = live_count(encode_target)
    encode_summed, encode_stored = edge_forward(
        grid_wide,
        encode_senders,
        encode_targets,
        encode_edges,
        encode_weight,
        mesh_rows,
        encode_blocks,
    )
    mesh_mid = (mesh_feats.astype(jnp.float32) + encode_factor * encode_summed).astype(jnp.bfloat16)
    fine_local = owner_fine - tile_id * level_rows
    fine_members = membership(fine_local, level_rows, jnp.bfloat16)
    middle_part = jnp.dot(fine_members, mesh_mid, preferred_element_type=jnp.float32)
    middle_sum = taken_together(middle_part, "sub")
    middle_in = (middle_factor * middle_sum).astype(jnp.bfloat16)
    middle_act = jnp.dot(middle_in, middle_weight, preferred_element_type=jnp.float32)
    middle_out = (middle_in.astype(jnp.float32) + jax.nn.silu(middle_act)).astype(jnp.bfloat16)
    top_members = membership(owner_coarse, TOP_NODES, jnp.bfloat16)
    summit_part = jnp.dot(top_members, middle_out, preferred_element_type=jnp.float32)
    summit_share = summed_on_arrival(summit_part, "tile", 0)
    summit_in = (summit_factor * summit_share).astype(jnp.bfloat16)
    summit_act = jnp.dot(summit_in, summit_weight, preferred_element_type=jnp.float32)
    summit_out = gather_directly(jax.nn.silu(summit_act).astype(jnp.bfloat16), "tile", 0)
    coarse_of = jnp.take(owner_coarse, fine_local)
    lifted = jnp.take(middle_out, fine_local, axis=0).astype(jnp.float32) + jnp.take(
        summit_out, coarse_of, axis=0
    ).astype(jnp.float32)
    mesh_out = (mesh_mid.astype(jnp.float32) + lifted).astype(jnp.bfloat16)
    mesh_wide = with_halo(mesh_out, ((("tile", "sub"), 0),), mesh_rows)
    decode_senders = decode_source - (device - 1) * mesh_rows
    decode_targets = local_targets(decode_target, device * grid_rows, grid_rows)
    decode_blocks = live_count(decode_target)
    decode_summed, decode_stored = edge_forward(
        mesh_wide,
        decode_senders,
        decode_targets,
        decode_edges,
        decode_weight,
        grid_rows,
        decode_blocks,
    )
    grid_update = (grid_feats.astype(jnp.float32) + decode_factor * decode_summed).astype(
        jnp.bfloat16
    )
    decode_local, decode_returned = edge_backward(
        mesh_wide,
        decode_senders,
        decode_targets,
        decode_stored,
        decode_weight,
        cotangent,
        decode_factor,
        decode_blocks,
        3 * mesh_rows,
    )
    from_next = from_behind(decode_returned[:mesh_rows], ("tile", "sub"), -1)
    from_prev = from_behind(decode_returned[2 * mesh_rows :], ("tile", "sub"), 1)
    mesh_grad = decode_returned[mesh_rows : 2 * mesh_rows] + from_next + from_prev
    level_part = exact_sum(fine_members.astype(jnp.float32), mesh_grad)
    level_grad = taken_together(level_part, "sub")
    summit_grad_part = exact_sum(top_members.astype(jnp.float32), level_grad)
    summit_grad_share = summed_on_arrival(summit_grad_part, "tile", 0)
    summit_slope = (summit_grad_share * silu_slope(summit_act)).astype(jnp.bfloat16)
    summit_local = outer_sum(summit_in, summit_slope)
    summit_back = gather_directly(
        times_transposed(summit_slope, summit_weight).astype(jnp.bfloat16), "tile", 0
    )
    level_total = level_grad + summit_factor * jnp.take(summit_back, owner_coarse, axis=0).astype(
        jnp.float32
    )
    middle_slope = (level_total * silu_slope(middle_act)).astype(jnp.bfloat16)
    middle_local = outer_sum(middle_in, middle_slope)
    middle_back = level_total + times_transposed(middle_slope, middle_weight)
    mesh_total = mesh_grad + middle_factor * jnp.take(middle_back, fine_local, axis=0)
    encode_local, unused_rows = edge_backward(
        grid_wide,
        encode_senders,
        encode_targets,
        encode_stored,
        encode_weight,
        mesh_total,
        encode_factor,
        encode_blocks,
        0,
    )
    sub_share = 1.0 / subs
    encode_grad, decode_grad, middle_grad, summit_grad = lax.psum(
        (encode_local, decode_local, sub_share * middle_local, sub_share * summit_local),
        ("tile", "sub"),
    )
    return (grid_update, encode_grad, decode_grad, middle_grad, summit_grad)


def solution(mesh):
    placed = (
        P(("tile", "sub"), None),
        P(("tile", "sub"), None),
        P(("tile", "sub"), None),
        P(("tile", "sub"), None),
        P(("tile", "sub")),
        P(("tile", "sub")),
        P(("tile", "sub")),
        P(("tile", "sub")),
        P(("tile", "sub")),
        P("tile"),
        P(),
        P(),
        P(),
        P(),
        P(("tile", "sub"), None),
    )
    return jax.shard_map(
        shards,
        mesh=mesh,
        in_specs=placed,
        out_specs=(P(("tile", "sub"), None), P(), P(), P(), P()),
        check_vma=False,
    )
```

profile of v0, /device:TPU:2, one launch (start us, length us, event | category | flops | bytes accessed | tf_op | source)
XLA Modules:
  0.0 638.4 jit_solution(1157762285381149726)
XLA Ops:
  7.2 2.1 collective-permute-start
  9.3 4.5 collective-permute-start.1
  15.2 1.4 convert_reduce_fusion
  17.5 1.6 broadcast_in_dim.117
  19.2 4.6 while.46
  20.8 1.9 constant_dynamic-update-slice_fusion.7
  24.2 41.1 %all_to_all.30 = f32[4,128,512]{2,1,0:T(8,128)S(1)} all-to-all(f32[4,128,512]{2,1,0:T(8,128)S(1)} %broadcast_in_dim.120), channel_id=1, replica_groups=mesh['tile'=64,'sub'=4] {'sub'}, dimensions={0} | all-to-all | bytes 2097152 | tf_op jit(solution)/shard_map/all_to_all | solution.py:32
  66.7 48.6 %all_to_all.31 = f32[64,8,512]{2,1,0:T(8,128)S(1)} all-to-all(f32[64,8,512]{2,1,0:T(8,128)S(1)} %convolution_bitcast_fusion), channel_id=1, replica_groups=mesh['tile'=64,'sub'=4] {'tile'}, dimensions={0} | all-to-all | bytes 2097152 | tf_op jit(solution)/shard_map/all_to_all | solution.py:47
  117.0 7.7 %all-to-all-start.2 = ((bf16[64,8,512]{2,1,0:T(8,128)(2,1)}), bf16[64,8,512]{2,1,0:T(8,128)(2,1)S(1)}, u32[]{:S(2)}, u32[]{:S(2)}) async-start(bf16[64,8,512]{2,1,0:T(8,128)(2,1)} %broadcast_in_dim.123), calls=%async_computation.2 | async-start | bytes 1048576 | tf_op jit(solution)/shard_map/all_to_all | solution.py:32
  126.9 14.6 %all-to-all-done.2 = bf16[64,8,512]{2,1,0:T(8,128)(2,1)S(1)} async-done(((bf16[64,8,512]{2,1,0:T(8,128)(2,1)}), bf16[64,8,512]{2,1,0:T(8,128)(2,1)S(1)}, u32[]{:S(2)}, u32[]{:S(2)}) %all-to-all-start.2) | async-done | bytes 524320 | tf_op jit(solution)/shard_map/all_to_all | solution.py:32
  142.5 1.9 collective-permute-start.2
  144.4 4.5 collective-permute-start.3
  152.4 25.7 %while.47 = (s32[]{:T(128)}, f32[128,512]{1,0:T(8,128)}, f32[512,512]{1,0:T(8,128)S(1)}, s32[]{:T(128)}, s32[512]{0:T(512)}, /*index=5*/s32[512]{0:T(512)}, bf16...) while((s32[]{:T(128)}, f32[128,512]{1,0:T(8,128)}, ...), condition=%wide.region_7.10_spmd, body=%wide.region_6.9_spmd.sunk | while | flops 168314624 | bytes 2367799 | solution.py:124
  156.7 2.0 convolution_add_fusion.14
  162.9 2.0 convolution_add_fusion.14
  169.2 2.0 convolution_add_fusion.14
  175.5 2.0 convolution_add_fusion.14
  179.3 29.3 %while.48 = (s32[]{:T(128)}, f32[512,512]{1,0:T(8,128)S(1)}, f32[384,512]{1,0:T(8,128)S(1)}, s32[]{:T(128)}, s32[512]{0:T(512)}, /*index=5*/bf16[384,512]{1,0:T(...) while((s32[]{:T(128)}, f32[512,512]{1,0:T(8,128)S(1)}, ...), condition=%wide.region_9.12_spmd, body=%wide.region_8.11_spmd.sunk | while | flops 438357888 | bytes 8272603 | solution.py:149
  180.0 1.4 compare_and_fusion.16
  183.1 1.5 convolution_add_fusion.15
  184.6 1.3 fusion.84
  187.2 1.4 compare_and_fusion.16
  190.2 1.5 convolution_add_fusion.15
  191.8 1.3 fusion.84
  194.3 1.4 compare_and_fusion.16
  197.4 1.5 convolution_add_fusion.15
  199.0 1.3 fusion.84
  201.5 1.4 compare_and_fusion.16
  204.6 1.5 convolution_add_fusion.15
  206.1 1.3 fusion.84
  208.7 1.9 collective-permute-start.4
  210.6 2.4 collective-permute-start.5
  213.1 1.5 collective-permute-done.4
  214.6 4.7 collective-permute-done.5
  221.9 4.3 all-to-all-start.3
  226.2 14.5 %all-to-all-done.3 = f32[4,128,512]{2,1,0:T(8,128)} async-done(((f32[4,128,512]{2,1,0:T(8,128)}), f32[4,128,512]{2,1,0:T(8,128)}, u32[]{:S(2)}, u32[]{:S(2)}) %all-to-all-start.3) | async-done | bytes 1048608 | tf_op jit(solution)/shard_map/all_to_all | solution.py:32
  240.7 1.3 reduce_sum.58
  242.7 46.5 %all_to_all.32 = f32[64,8,512]{2,1,0:T(8,128)S(1)} all-to-all(f32[64,8,512]{2,1,0:T(8,128)S(1)} %fusion.42), channel_id=1, replica_groups=mesh['tile'=64,'sub'=4] {'tile'}, dimensions={0} | all-to-all | bytes 2097152 | tf_op jit(solution)/shard_map/all_to_all | solution.py:47
  289.3 1.3 convolution_convert_fusion
  291.5 7.7 %all-to-all-start.5 = ((bf16[64,8,512]{2,1,0:T(8,128)(2,1)}), bf16[64,8,512]{2,1,0:T(8,128)(2,1)S(1)}, u32[]{:S(2)}, u32[]{:S(2)}) async-start(bf16[64,8,512]{2,1,0:T(8,128)(2,1)} %broadcast_in_dim.127), calls=%async_computation.5 | async-start | bytes 1048576 | tf_op jit(solution)/shard_map/all_to_all | solution.py:32
  299.3 1.3 convolution_multiply_fusion
  300.6 15.4 %all-to-all-done.5 = bf16[64,8,512]{2,1,0:T(8,128)(2,1)S(1)} async-done(((bf16[64,8,512]{2,1,0:T(8,128)(2,1)}), bf16[64,8,512]{2,1,0:T(8,128)(2,1)S(1)}, u32[]{:S(2)}, u32[]{:S(2)}) %all-to-all-start.5) | async-done | bytes 524320 | tf_op jit(solution)/shard_map/all_to_all | solution.py:32
  316.9 1.4 convolution_multiply_fusion.1
  318.3 1.3 convolution_add_fusion.7
  320.8 5.2 while.49
  323.8 1.5 convolution_add_fusion.17
  328.0 298.2 %all-reduce.3.cloned.1.call-done = (f32[512,512]{1,0:T(8,128)}, f32[512,512]{1,0:T(8,128)}, f32[512,512]{1,0:T(8,128)}, f32[512,512]{1,0:T(8,128)}) async-done(((f32[512,512]{1,0:T(8,128)}, f32[512,512]{1,0:T(8,128)}, f32[512,512]{1,0:T(8,128)}, f32[512,512]{1,0:T(8,128)}), (f32[512,512]{1,0:T(8,128)}, f32[512,512]{1,0:T(8,128)}, f32[512,512]{1,0:T(8,128)}, ...) | async-done | bytes 4194320 | tf_op jit(solution)/shard_map/psum | solution.py:270
  626.2 2.4 copy.69
  (181 shorter events, 52.0 us)
Async XLA Ops:
  7.2 58.3 %copy-start = (bf16[512,512]{1,0:T(8,128)(2,1)S(1)}, bf16[512,512]{1,0:T(8,128)(2,1)}, u32[]{:S(2)}) copy-start(bf16[512,512]{1,0:T(8,128)(2,1)} %param.39) | copy-start | bytes 1572868
  7.2 12.0 %copy-start.5 = (bf16[512,512]{1,0:T(8,128)(2,1)S(1)}, bf16[512,512]{1,0:T(8,128)(2,1)}, u32[]{:S(2)}) copy-start(bf16[512,512]{1,0:T(8,128)(2,1)} %param.37) | copy-start | bytes 1572868
  7.2 9.4 %collective-permute-start = (bf16[128,512]{1,0:T(8,128)(2,1)}, bf16[128,512]{1,0:T(8,128)(2,1)S(1)}, u32[]{:S(2)}, u32[]{:S(2)}) collective-permute-start(bf16[128,512]{1,0:T(8,128)(2,1)} %param.27), channel_id=1, source_target_pairs={{0,1},{1,2},{2,3},{3,4},{4,5},{5,6},{6,7},{7,8},{8,9},{9,10},{10,1... | collective-permute-start | bytes 393224 | tf_op jit(solution)/shard_map/ppermute | solution.py:18
  9.3 8.2 %collective-permute-start.1 = (bf16[128,512]{1,0:T(8,128)(2,1)}, bf16[128,512]{1,0:T(8,128)(2,1)S(1)}, u32[]{:S(2)}, u32[]{:S(2)}) collective-permute-start(bf16[128,512]{1,0:T(8,128)(2,1)} %param.27), channel_id=1, source_target_pairs={{1,0},{2,1},{3,2},{4,3},{5,4},{6,5},{7,6},{8,7},{9,8},{10,9},{11,1... | collective-permute-start | bytes 393224 | tf_op jit(solution)/shard_map/ppermute | solution.py:19
  15.2 110.8 %copy-start.28 = (s32[128]{0:T(128)}, s32[128]{0:T(128)S(1)}, u32[]{:S(2)}) copy-start(s32[128]{0:T(128)S(1)} %get-tuple-element.301) | copy-start | bytes 1540
  19.2 4.7 copy-start.19
  23.8 41.6 %copy-start.25 = (s32[1024]{0:T(1024)}, s32[1024]{0:T(1024)S(1)}, u32[]{:S(2)}) copy-start(s32[1024]{0:T(1024)S(1)} %get-tuple-element.774) | copy-start | bytes 12292
  23.8 41.6 %copy-start.26 = (s32[1024]{0:T(1024)}, s32[1024]{0:T(1024)S(1)}, u32[]{:S(2)}) copy-start(s32[1024]{0:T(1024)S(1)} %get-tuple-element.775) | copy-start | bytes 12292
  24.2 42.2 %copy-start.1 = (s32[128]{0:T(128)S(1)}, s32[128]{0:T(128)}, u32[]{:S(2)}) copy-start(s32[128]{0:T(128)} %param.36) | copy-start | bytes 1540
  65.4 1.0 copy-start.20
  66.4 49.0 %copy-start.9 = (bf16[512,512]{1,0:T(8,128)(2,1)S(1)}, bf16[512,512]{1,0:T(8,128)(2,1)}, u32[]{:S(2)}) copy-start(bf16[512,512]{1,0:T(8,128)(2,1)} %param.40) | copy-start | bytes 1572868
  115.4 1.6 copy-start.22
  117.0 24.5 %all-to-all-start.2 = ((bf16[64,8,512]{2,1,0:T(8,128)(2,1)}), bf16[64,8,512]{2,1,0:T(8,128)(2,1)S(1)}, u32[]{:S(2)}, u32[]{:S(2)}) async-start(bf16[64,8,512]{2,1,0:T(8,128)(2,1)} %broadcast_in_dim.123), calls=%async_computation.2 | async-start | bytes 1048576 | tf_op jit(solution)/shard_map/all_to_all | solution.py:32
  124.7 24.3 %copy-start.27 = (s32[512]{0:T(512)S(1)}, s32[512]{0:T(512)}, u32[]{:S(2)}) copy-start(s32[512]{0:T(512)} %param.34) | copy-start | bytes 6148
  124.7 24.3 %copy-start.32 = (s32[512]{0:T(512)S(1)}, s32[512]{0:T(512)}, u32[]{:S(2)}) copy-start(s32[512]{0:T(512)} %param.33) | copy-start | bytes 6148
  124.8 26.7 %copy-start.29 = (s32[1024]{0:T(1024)}, s32[1024]{0:T(1024)S(1)}, u32[]{:S(2)}) copy-start(s32[1024]{0:T(1024)S(1)} %pad_clamp_fusion.8) | copy-start | bytes 12292
  126.0 24.3 %copy-start.30 = (pred[128]{0:T(512)(128)(4,1)}, pred[128]{0:T(512)(128)(4,1)S(1)}, u32[]{:S(2)}) copy-start(pred[128]{0:T(512)(128)(4,1)S(1)} %get-tuple-element.299) | copy-start | bytes 388
  126.9 25.5 %copy-start.6 = (bf16[512,512]{1,0:T(8,128)(2,1)S(1)}, bf16[512,512]{1,0:T(8,128)(2,1)}, u32[]{:S(2)}) copy-start(bf16[512,512]{1,0:T(8,128)(2,1)} %param.38) | copy-start | bytes 1572868
  142.5 7.8 %collective-permute-start.2 = (bf16[128,512]{1,0:T(8,128)(2,1)S(1)}, bf16[128,512]{1,0:T(8,128)(2,1)S(1)}, u32[]{:S(2)}, u32[]{:S(2)}) collective-permute-start(bf16[128,512]{1,0:T(8,128)(2,1)S(1)} %add_convert_fusion.1), channel_id=1, source_target_pairs={{0,1},{1,2},{2,3},{3,4},{4,5},{5,6},{6,7},{7,8},{8,9},{9,10},{10,1... | collective-permute-start | bytes 393224 | tf_op jit(solution)/shard_map/ppermute | solution.py:18
  144.4 7.0 %collective-permute-start.3 = (bf16[128,512]{1,0:T(8,128)(2,1)S(1)}, bf16[128,512]{1,0:T(8,128)(2,1)S(1)}, u32[]{:S(2)}, u32[]{:S(2)}) collective-permute-start(bf16[128,512]{1,0:T(8,128)(2,1)S(1)} %add_convert_fusion.1), channel_id=1, source_target_pairs={{1,0},{2,1},{3,2},{4,3},{5,4},{6,5},{7,6},{8,7},{9,8},{10,9},{11,1... | collective-permute-start | bytes 393224 | tf_op jit(solution)/shard_map/ppermute | solution.py:19
  152.4 26.9 %copy-start.2 = (bf16[128,512]{1,0:T(8,128)(2,1)S(1)}, bf16[128,512]{1,0:T(8,128)(2,1)}, u32[]{:S(2)}) copy-start(bf16[128,512]{1,0:T(8,128)(2,1)} %param.41) | copy-start | bytes 393220
  178.1 1.0 copy-start.8
  183.1 1.5 copy-start.7
  190.2 1.5 copy-start.7
  197.4 1.5 copy-start.7
  204.6 1.5 copy-start.7
  208.7 13.3 %copy-start.3 = (f32[512,512]{1,0:T(8,128)}, f32[512,512]{1,0:T(8,128)S(1)}, u32[]{:S(2)}) copy-start(f32[512,512]{1,0:T(8,128)S(1)} %get-tuple-element.208) | copy-start | bytes 3145732
  208.7 5.8 collective-permute-start.4
  210.6 8.6 %collective-permute-start.5 = (f32[128,512]{1,0:T(8,128)S(1)}, f32[128,512]{1,0:T(8,128)S(1)}, u32[]{:S(2)}, u32[]{:S(2)}) collective-permute-start(f32[128,512]{1,0:T(8,128)S(1)} %get-tuple-element.311), channel_id=1, source_target_pairs={{0,1},{1,2},{2,3},{3,4},{4,5},{5,6},{6,7},{7,8},{8,9},{9,10},{10,1... | collective-permute-start | bytes 786440 | tf_op jit(solution)/shard_map/ppermute | solution.py:64
  214.6 7.4 %copy-start.13 = (f32[128,512]{1,0:T(8,128)}, f32[128,512]{1,0:T(8,128)S(1)}, u32[]{:S(2)}) copy-start(f32[128,512]{1,0:T(8,128)S(1)} %collective-permute-done.4) | copy-start | bytes 786436
  219.2 0.7 copy-start.15
  221.9 18.8 %all-to-all-start.3 = ((f32[4,128,512]{2,1,0:T(8,128)}), f32[4,128,512]{2,1,0:T(8,128)}, u32[]{:S(2)}, u32[]{:S(2)}) async-start(f32[4,128,512]{2,1,0:T(8,128)} %broadcast_in_dim.126), calls=%async_computation.3 | async-start | bytes 2097152 | tf_op jit(solution)/shard_map/all_to_all | solution.py:32
  242.0 47.2 %copy-start.24 = (f32[8,512]{1,0:T(8,128)S(1)}, f32[8,512]{1,0:T(8,128)}, u32[]{:S(2)}) copy-start(f32[8,512]{1,0:T(8,128)} %get-tuple-element.315) | copy-start | bytes 49156
  289.2 10.1 %copy-start.23 = (f32[8,512]{1,0:T(8,128)S(1)}, f32[8,512]{1,0:T(8,128)}, u32[]{:S(2)}) copy-start(f32[8,512]{1,0:T(8,128)} %copy-done.22) | copy-start | bytes 49156
  289.3 27.6 %copy-start.21 = (f32[128,512]{1,0:T(8,128)S(1)}, f32[128,512]{1,0:T(8,128)}, u32[]{:S(2)}) copy-start(f32[128,512]{1,0:T(8,128)} %copy-done.20) | copy-start | bytes 786436
  289.3 27.6 %copy-start.33 = (f32[128,512]{1,0:T(8,128)S(1)}, f32[128,512]{1,0:T(8,128)}, u32[]{:S(2)}) copy-start(f32[128,512]{1,0:T(8,128)} %get-tuple-element.313) | copy-start | bytes 786436
  291.5 24.5 %all-to-all-start.5 = ((bf16[64,8,512]{2,1,0:T(8,128)(2,1)}), bf16[64,8,512]{2,1,0:T(8,128)(2,1)S(1)}, u32[]{:S(2)}, u32[]{:S(2)}) async-start(bf16[64,8,512]{2,1,0:T(8,128)(2,1)} %broadcast_in_dim.127), calls=%async_computation.5 | async-start | bytes 1048576 | tf_op jit(solution)/shard_map/all_to_all | solution.py:32
  299.2 327.0 %all-reduce.3.cloned.1.call-start = ((), (), s32[]{:S(2)}) async-start(), calls=%async_computation.6 | async-start | bytes 8388608 | tf_op jit(solution)/shard_map/psum | solution.py:270
  318.3 2.2 copy-start.14
  318.3 2.2 copy-start.16
  318.3 2.2 copy-start.31
  326.0 1.0 copy-start.4
  326.0 1.1 copy-start.17
  326.0 1.3 copy-start.18
  626.2 2.4 copy-start.12
  626.2 3.4 copy-start.11
  628.6 1.9 copy-start.10
Sparse Core Ops, SparseCore 0:
  327.1 299.0 all-reduce.2
where the time goes:
time: 641 us; the launch traced here: 638 us
  waiting for transfers between devices  350 us (55%)
  blocking collectives  136 us (21%)
  matrix products  39.3 us (6%)
  starting transfers between devices  37.1 us (6%)
  local copies, waits for them, and re-layouts  35.5 us (6%)
  other arithmetic  16.1 us (3%)
  between operations  14.7 us (2%)
  loops' own time  9.42 us (1%)
    psum x1, waiting for transfers between devices, shards(): lax.psum((encode_local, decode_local, sub_share * middle_local, sub_share...  298 us
    all_to_all x2, blocking collectives, summed_on_arrival(): lax.all_to_all(pieces, axis, split_axis=0, concat_axis=0, tiled=True)  95.1 us
    all_to_all x3, waiting for transfers between devices, copy_for_each(): lax.all_to_all(jnp.broadcast_to(x[None], (peers, *x.shape)), axis, 0, 0,...  44.5 us
    all_to_all x1, blocking collectives, copy_for_each(): lax.all_to_all(jnp.broadcast_to(x[None], (peers, *x.shape)), axis, 0, 0,...  41.1 us
    all_to_all x3, starting transfers between devices, copy_for_each(): lax.all_to_all(jnp.broadcast_to(x[None], (peers, *x.shape)), axis, 0, 0,...  19.7 us
  transfers between devices with their start and end apart: 10, of which 7 were waited for; matrix products, arithmetic and copies ran while one was open for 1% of the time, Pallas kernels for 0%

commit v1 on v0

--- a/solution.py
+++ b/solution.py
@@ -268,8 +268,10 @@
     )
     sub_share = 1.0 / subs
     encode_grad, decode_grad, middle_grad, summit_grad = lax.psum(
-        (encode_local, decode_local, sub_share * middle_local, sub_share * summit_local),
-        ("tile", "sub"),
+        lax.psum(
+            (encode_local, decode_local, sub_share * middle_local, sub_share * summit_local), "tile"
+        ),
+        "sub",
     )
     return (grid_update, encode_grad, decode_grad, middle_grad, summit_grad)
 

time: 641 us -> 1180 us (1.84)
  waiting for transfers between devices: 350 us -> 885 us
    psum x1, waiting for transfers between devices: 298 us -> 737 us  [shards(): lax.psum((encode_local, decode_local, sub_share * middle_local, sub_share...]
    psum x0 -> x1, waiting for transfers between devices: none -> 96.2 us  [shards(): lax.psum(lax.psum((encode_local, decode_local, sub_share * middle_local,...]
  transfers between devices with their start and end apart: 10 -> 11, of which waited for: 7 -> 8; matrix products, arithmetic and copies ran while one was open for 1% -> 1% of each run, Pallas kernels for 0% -> 0%
where the time goes in v1:
time: 1180 us; the launch traced here: 1170 us
  waiting for transfers between devices  885 us (75%)
  blocking collectives  136 us (12%)
  matrix products  39.3 us (3%)
  starting transfers between devices  37.2 us (3%)
  local copies, waits for them, and re-layouts  36.1 us (3%)
  other arithmetic  15.9 us (1%)
  between operations  14.7 us (1%)
    psum x1, waiting for transfers between devices, shards(): lax.psum((encode_local, decode_local, sub_share * middle_local, sub_share...  737 us
    psum x1, waiting for transfers between devices, shards(): lax.psum(lax.psum((encode_local, decode_local, sub_share * middle_local,...  96.2 us
    all_to_all x2, blocking collectives, summed_on_arrival(): lax.all_to_all(pieces, axis, split_axis=0, concat_axis=0, tiled=True)  95.1 us
    all_to_all x3, waiting for transfers between devices, copy_for_each(): lax.all_to_all(jnp.broadcast_to(x[None], (peers, *x.shape)), axis, 0, 0,...  44.5 us
    all_to_all x1, blocking collectives, copy_for_each(): lax.all_to_all(jnp.broadcast_to(x[None], (peers, *x.shape)), axis, 0, 0,...  41.2 us
  transfers between devices with their start and end apart: 11, of which 8 were waited for; matrix products, arithmetic and copies ran while one was open for 1% of the time, Pallas kernels for 0%

profile of v1, /device:TPU:2, one launch (start us, length us, event | category | flops | bytes accessed | tf_op | source)
XLA Modules:
  0.0 1173.2 jit_solution(12485432320474309441)
XLA Ops:
  7.2 2.1 collective-permute-start
  9.3 4.5 collective-permute-start.1
  15.2 1.3 convert_reduce_fusion
  17.5 1.6 broadcast_in_dim.117
  19.1 4.6 while.46
  20.8 1.9 constant_dynamic-update-slice_fusion.7
  24.1 41.2 %all_to_all.30 = f32[4,128,512]{2,1,0:T(8,128)S(1)} all-to-all(f32[4,128,512]{2,1,0:T(8,128)S(1)} %broadcast_in_dim.120), channel_id=1, replica_groups=mesh['tile'=64,'sub'=4] {'sub'}, dimensions={0} | all-to-all | bytes 2097152 | tf_op jit(solution)/shard_map/all_to_all | solution.py:32
  66.6 48.6 %all_to_all.31 = f32[64,8,512]{2,1,0:T(8,128)S(1)} all-to-all(f32[64,8,512]{2,1,0:T(8,128)S(1)} %convolution_bitcast_fusion), channel_id=1, replica_groups=mesh['tile'=64,'sub'=4] {'tile'}, dimensions={0} | all-to-all | bytes 2097152 | tf_op jit(solution)/shard_map/all_to_all | solution.py:47
  117.0 7.7 all-to-all-start.2
  126.9 14.6 %all-to-all-done.2 = bf16[64,8,512]{2,1,0:T(8,128)(2,1)S(1)} async-done(((bf16[64,8,512]{2,1,0:T(8,128)(2,1)}), bf16[64,8,512]{2,1,0:T(8,128)(2,1)S(1)}, u32[]{:S(2)}, u32[]{:S(2)}) %all-to-all-start.2) | async-done | bytes 524320 | tf_op jit(solution)/shard_map/all_to_all | solution.py:32
  142.5 1.9 collective-permute-start.2
  144.4 4.5 collective-permute-start.3
  152.4 25.3 %while.47 = (s32[]{:T(128)}, f32[128,512]{1,0:T(8,128)}, f32[512,512]{1,0:T(8,128)S(1)}, s32[]{:T(128)}, s32[512]{0:T(512)}, /*index=5*/s32[512]{0:T(512)}, bf16...) while((s32[]{:T(128)}, f32[128,512]{1,0:T(8,128)}, ...), condition=%wide.region_7.10_spmd, body=%wide.region_6.9_spmd.sunk | while | flops 168314624 | bytes 2367799 | solution.py:124
  156.5 2.0 convolution_add_fusion.14
  162.7 2.0 convolution_add_fusion.14
  168.9 2.0 convolution_add_fusion.14
  175.1 2.0 convolution_add_fusion.14
  178.9 29.0 %while.48 = (s32[]{:T(128)}, f32[512,512]{1,0:T(8,128)S(1)}, f32[384,512]{1,0:T(8,128)S(1)}, s32[]{:T(128)}, s32[512]{0:T(512)}, /*index=5*/bf16[384,512]{1,0:T(...) while((s32[]{:T(128)}, f32[512,512]{1,0:T(8,128)S(1)}, ...), condition=%wide.region_9.12_spmd, body=%wide.region_8.11_spmd.sunk | while | flops 438357888 | bytes 8272603 | solution.py:149
  179.5 1.3 compare_and_fusion.16
  182.6 1.5 convolution_add_fusion.15
  184.1 1.3 fusion.84
  186.6 1.3 compare_and_fusion.16
  189.7 1.5 convolution_add_fusion.15
  191.2 1.3 fusion.84
  193.7 1.3 compare_and_fusion.16
  196.8 1.5 convolution_add_fusion.15
  200.8 1.3 compare_and_fusion.16
  203.9 1.5 convolution_add_fusion.15
  205.4 1.3 fusion.84
  207.9 1.9 collective-permute-start.4
  209.8 2.4 collective-permute-start.5
  212.3 1.5 collective-permute-done.4
  213.8 4.7 collective-permute-done.5
  221.2 4.3 all-to-all-start.3
  225.5 14.5 %all-to-all-done.3 = f32[4,128,512]{2,1,0:T(8,128)} async-done(((f32[4,128,512]{2,1,0:T(8,128)}), f32[4,128,512]{2,1,0:T(8,128)}, u32[]{:S(2)}, u32[]{:S(2)}) %all-to-all-start.3) | async-done | bytes 1048608 | tf_op jit(solution)/shard_map/all_to_all | solution.py:32
  240.0 1.3 reduce_sum.58
  242.0 46.5 %all_to_all.32 = f32[64,8,512]{2,1,0:T(8,128)S(1)} all-to-all(f32[64,8,512]{2,1,0:T(8,128)S(1)} %fusion.42), channel_id=1, replica_groups=mesh['tile'=64,'sub'=4] {'tile'}, dimensions={0} | all-to-all | bytes 2097152 | tf_op jit(solution)/shard_map/all_to_all | solution.py:47
  288.6 1.3 convolution_convert_fusion
  290.8 7.7 all-to-all-start.5
  298.6 1.3 convolution_multiply_fusion
  299.9 15.4 %all-to-all-done.5 = bf16[64,8,512]{2,1,0:T(8,128)(2,1)S(1)} async-done(((bf16[64,8,512]{2,1,0:T(8,128)(2,1)}), bf16[64,8,512]{2,1,0:T(8,128)(2,1)S(1)}, u32[]{:S(2)}, u32[]{:S(2)}) %all-to-all-start.5) | async-done | bytes 524320 | tf_op jit(solution)/shard_map/all_to_all | solution.py:32
  316.2 1.4 convolution_multiply_fusion.1
  317.6 1.3 convolution_add_fusion.7
  320.0 5.2 while.49
  323.1 1.5 convolution_add_fusion.17
  326.3 736.9 %all-reduce.5.cloned.1.call-done = (f32[512,512]{1,0:T(8,128)}, f32[512,512]{1,0:T(8,128)}, f32[512,512]{1,0:T(8,128)}, f32[512,512]{1,0:T(8,128)}) async-done(((f32[512,512]{1,0:T(8,128)}, f32[512,512]{1,0:T(8,128)}, f32[512,512]{1,0:T(8,128)}, f32[512,512]{1,0:T(8,128)}), (f32[512,512]{1,0:T(8,128)}, f32[512,512]{1,0:T(8,128)}, f32[512,512]{1,0:T(8,128)}, ...) | async-done | bytes 4194320 | tf_op jit(solution)/shard_map/psum | solution.py:271
  1064.8 96.2 %all-reduce.7.cloned.1.call-done = (f32[512,512]{1,0:T(8,128)}, f32[512,512]{1,0:T(8,128)}, f32[512,512]{1,0:T(8,128)}, f32[512,512]{1,0:T(8,128)}) async-done(((f32[512,512]{1,0:T(8,128)}, f32[512,512]{1,0:T(8,128)}, f32[512,512]{1,0:T(8,128)}, f32[512,512]{1,0:T(8,128)}), (f32[512,512]{1,0:T(8,128)}, f32[512,512]{1,0:T(8,128)}, f32[512,512]{1,0:T(8,128)}, ...) | async-done | bytes 4194320 | tf_op jit(solution)/shard_map/psum | solution.py:270
  1161.0 2.4 copy.73
  (184 shorter events, 54.0 us)
Async XLA Ops:
  7.2 58.2 %copy-start = (bf16[512,512]{1,0:T(8,128)(2,1)S(1)}, bf16[512,512]{1,0:T(8,128)(2,1)}, u32[]{:S(2)}) copy-start(bf16[512,512]{1,0:T(8,128)(2,1)} %param.39) | copy-start | bytes 1572868
  7.2 11.9 %copy-start.5 = (bf16[512,512]{1,0:T(8,128)(2,1)S(1)}, bf16[512,512]{1,0:T(8,128)(2,1)}, u32[]{:S(2)}) copy-start(bf16[512,512]{1,0:T(8,128)(2,1)} %param.37) | copy-start | bytes 1572868
  7.2 9.3 collective-permute-start
  9.3 8.2 collective-permute-start.1
  15.2 110.8 %copy-start.28 = (s32[128]{0:T(128)}, s32[128]{0:T(128)S(1)}, u32[]{:S(2)}) copy-start(s32[128]{0:T(128)S(1)} %get-tuple-element.305) | copy-start | bytes 1540
  19.1 4.7 copy-start.19
  23.8 41.6 %copy-start.25 = (s32[1024]{0:T(1024)}, s32[1024]{0:T(1024)S(1)}, u32[]{:S(2)}) copy-start(s32[1024]{0:T(1024)S(1)} %get-tuple-element.796) | copy-start | bytes 12292
  23.8 41.6 %copy-start.26 = (s32[1024]{0:T(1024)}, s32[1024]{0:T(1024)S(1)}, u32[]{:S(2)}) copy-start(s32[1024]{0:T(1024)S(1)} %get-tuple-element.797) | copy-start | bytes 12292
  24.1 42.3 %copy-start.1 = (s32[128]{0:T(128)S(1)}, s32[128]{0:T(128)}, u32[]{:S(2)}) copy-start(s32[128]{0:T(128)} %param.36) | copy-start | bytes 1540
  65.4 1.0 copy-start.20
  66.4 49.0 %copy-start.9 = (bf16[512,512]{1,0:T(8,128)(2,1)S(1)}, bf16[512,512]{1,0:T(8,128)(2,1)}, u32[]{:S(2)}) copy-start(bf16[512,512]{1,0:T(8,128)(2,1)} %param.40) | copy-start | bytes 1572868
  115.3 1.6 copy-start.22
  117.0 24.5 %all-to-all-start.2 = ((bf16[64,8,512]{2,1,0:T(8,128)(2,1)}), bf16[64,8,512]{2,1,0:T(8,128)(2,1)S(1)}, u32[]{:S(2)}, u32[]{:S(2)}) async-start(bf16[64,8,512]{2,1,0:T(8,128)(2,1)} %broadcast_in_dim.123), calls=%async_computation.2 | async-start | bytes 1048576 | tf_op jit(solution)/shard_map/all_to_all | solution.py:32
  124.7 24.3 %copy-start.27 = (s32[512]{0:T(512)S(1)}, s32[512]{0:T(512)}, u32[]{:S(2)}) copy-start(s32[512]{0:T(512)} %param.34) | copy-start | bytes 6148
  124.7 24.3 %copy-start.32 = (s32[512]{0:T(512)S(1)}, s32[512]{0:T(512)}, u32[]{:S(2)}) copy-start(s32[512]{0:T(512)} %param.33) | copy-start | bytes 6148
  124.7 26.7 %copy-start.29 = (s32[1024]{0:T(1024)}, s32[1024]{0:T(1024)S(1)}, u32[]{:S(2)}) copy-start(s32[1024]{0:T(1024)S(1)} %pad_clamp_fusion.8) | copy-start | bytes 12292
  126.0 24.2 %copy-start.30 = (pred[128]{0:T(512)(128)(4,1)}, pred[128]{0:T(512)(128)(4,1)S(1)}, u32[]{:S(2)}) copy-start(pred[128]{0:T(512)(128)(4,1)S(1)} %get-tuple-element.303) | copy-start | bytes 388
  126.9 25.5 %copy-start.6 = (bf16[512,512]{1,0:T(8,128)(2,1)S(1)}, bf16[512,512]{1,0:T(8,128)(2,1)}, u32[]{:S(2)}) copy-start(bf16[512,512]{1,0:T(8,128)(2,1)} %param.38) | copy-start | bytes 1572868
  142.5 7.7 collective-permute-start.2
  144.4 7.0 collective-permute-start.3
  152.4 26.5 %copy-start.2 = (bf16[128,512]{1,0:T(8,128)(2,1)S(1)}, bf16[128,512]{1,0:T(8,128)(2,1)}, u32[]{:S(2)}) copy-start(bf16[128,512]{1,0:T(8,128)(2,1)} %param.41) | copy-start | bytes 393220
  177.7 1.0 copy-start.8
  182.5 1.5 copy-start.7
  189.6 1.5 copy-start.7
  196.7 1.5 copy-start.7
  203.8 1.5 copy-start.7
  207.9 13.3 %copy-start.3 = (f32[512,512]{1,0:T(8,128)}, f32[512,512]{1,0:T(8,128)S(1)}, u32[]{:S(2)}) copy-start(f32[512,512]{1,0:T(8,128)S(1)} %get-tuple-element.208) | copy-start | bytes 3145732
  207.9 5.8 collective-permute-start.4
  209.8 8.6 collective-permute-start.5
  213.8 7.5 copy-start.13
  218.4 0.7 copy-start.15
  221.2 18.8 %all-to-all-start.3 = ((f32[4,128,512]{2,1,0:T(8,128)}), f32[4,128,512]{2,1,0:T(8,128)}, u32[]{:S(2)}, u32[]{:S(2)}) async-start(f32[4,128,512]{2,1,0:T(8,128)} %broadcast_in_dim.126), calls=%async_computation.3 | async-start | bytes 2097152 | tf_op jit(solution)/shard_map/all_to_all | solution.py:32
  241.3 47.2 %copy-start.24 = (f32[8,512]{1,0:T(8,128)S(1)}, f32[8,512]{1,0:T(8,128)}, u32[]{:S(2)}) copy-start(f32[8,512]{1,0:T(8,128)} %get-tuple-element.319) | copy-start | bytes 49156
  288.4 10.1 copy-start.23
  288.6 27.6 %copy-start.21 = (f32[128,512]{1,0:T(8,128)S(1)}, f32[128,512]{1,0:T(8,128)}, u32[]{:S(2)}) copy-start(f32[128,512]{1,0:T(8,128)} %copy-done.20) | copy-start | bytes 786436
  288.6 27.6 %copy-start.33 = (f32[128,512]{1,0:T(8,128)S(1)}, f32[128,512]{1,0:T(8,128)}, u32[]{:S(2)}) copy-start(f32[128,512]{1,0:T(8,128)} %get-tuple-element.317) | copy-start | bytes 786436
  290.8 24.5 %all-to-all-start.5 = ((bf16[64,8,512]{2,1,0:T(8,128)(2,1)}), bf16[64,8,512]{2,1,0:T(8,128)(2,1)S(1)}, u32[]{:S(2)}, u32[]{:S(2)}) async-start(bf16[64,8,512]{2,1,0:T(8,128)(2,1)} %broadcast_in_dim.127), calls=%async_computation.5 | async-start | bytes 1048576 | tf_op jit(solution)/shard_map/all_to_all | solution.py:32
  298.5 764.6 %all-reduce.5.cloned.1.call-start = ((), (), s32[]{:S(2)}) async-start(), calls=%async_computation.6 | async-start | bytes 8388608 | tf_op jit(solution)/shard_map/psum | solution.py:271
  317.6 2.2 copy-start.14
  317.6 2.2 copy-start.16
  317.6 2.2 copy-start.31
  325.2 1.0 copy-start.4
  326.2 834.8 %all-reduce.7.cloned.1.call-start = ((), (), s32[]{:S(2)}) async-start(), calls=%async_computation.7 | async-start | bytes 8388608 | tf_op jit(solution)/shard_map/psum | solution.py:270
  1063.1 0.9 copy-start.17
  1063.2 1.0 copy-start.18
  1161.0 2.4 copy-start.12
  1161.0 3.4 copy-start.11
  1163.5 1.9 copy-start.10
Sparse Core Ops, SparseCore 0:
  326.3 736.7 all-reduce.4
  1066.0 94.9 all-reduce.6
